TPU v7x, 32 devices: a whole 2x2x4 slice. The times are simulated.
32 devices in a mesh: batch: 4 (over y, x), ctx: 8 (over z, core).
Axes of the slice: x: 2, y: 2, z: 4, core: 2. Of those that a mesh axis runs over, the one named last changes fastest.
Arguments:
- asked_for: bfloat16 [4, 1024, 64, 64], P('batch', 'ctx'), may hold values from -6 to 6
- offered: bfloat16 [4, 1024, 64, 64], P('batch', 'ctx'), may hold values from -6 to 6
- contents: bfloat16 [4, 1024, 64, 64], P('batch', 'ctx'), may hold values from -6 to 6
- out_weight: bfloat16 [4096, 4096], P('batch'), may hold values from -0.09375 to 0.09375
Outputs:
- layer_out: bfloat16 [4, 1024, 4096], P('batch', 'ctx')
All inputs are finite; a program needn't handle non-finite values.
Results may differ from a plain program's by a relative error of at most 0.006.
Values may be sent and summed in bfloat16 or wider, within the bound.
A program may use at most 128 MiB of HBM per device.

v0:
```python
import functools
import math

import jax
import jax.numpy as jnp
from jax import lax
from jax.experimental import pallas as pl
from jax.experimental.pallas import tpu as pltpu
from jax.sharding import PartitionSpec as P

MESH = pl.DeviceIdType.MESH
LANES = 128
EXTRA = 16
CHUNK = 512


def softplus(x):
    x = x.astype(jnp.float32)
    return (jnp.maximum(x, 0.0) + jnp.log(1.0 + jnp.exp(-jnp.abs(x)))).astype(jnp.bfloat16)


def split_mass(m):
    row = lax.broadcasted_iota(jnp.int32, (EXTRA, LANES), 0)
    high = m.astype(jnp.bfloat16).astype(jnp.float32)
    return jnp.where(row == 0, high, jnp.where(row == 1, m - high, 0.0)).astype(jnp.bfloat16)


def kernel(
    ny, nx, nc, size, q_ref, k_ref, v_ref, w_ref, o_ref,
    kt, vt, wv, qx, part, part_in, both, rs, own, st, mixed, mine, stage1, stage2,
    local_sem, q_send, q_recv, pa_send, pa_recv, rs_send, rs_recv,
    ag_send, ag_recv, fw_send, fw_recv,
):
    b, c = lax.axis_index("batch"), lax.axis_index("ctx")
    nb = ny * nx
    rows, tokens = k_ref.shape
    pairs = rows // LANES
    ppg, ppd = pairs // nb, pairs // nc
    group = rows // nb
    total = nb * nc
    me = b * nc + c
    count = tokens * nc
    chunks = mine[0].shape[0]

    barrier = pltpu.get_barrier_semaphore()

    def greet(i, carry):
        d = lax.rem(me + i, total)
        pl.semaphore_signal(barrier, inc=1, device_id=(d // nc, lax.rem(d, nc)), device_id_type=MESH)
        return carry

    lax.fori_loop(1, total, greet, 0)
    k_copy = pltpu.make_async_copy(k_ref, kt, local_sem.at[0])
    v_copy = pltpu.make_async_copy(v_ref, vt, local_sem.at[1])
    q_copy = pltpu.make_async_copy(q_ref.at[pl.ds(b * group, group)], qx.at[0], local_sem.at[2])
    w_copy = pltpu.make_async_copy(w_ref, wv, local_sem.at[3])
    k_copy.start()
    v_copy.start()
    q_copy.start()
    w_copy.start()
    pl.semaphore_wait(barrier, total - 1)

    y_me, x_me = b // nx, lax.rem(b, nx)

    def ahead(k):
        return lax.rem(y_me + k // nx, ny) * nx + lax.rem(x_me + k % nx, nx)

    def back(k):
        return (ny - k // nx) % ny * nx + (nx - k % nx) % nx

    def q_move(k):
        to = ahead(k)
        return pltpu.make_async_remote_copy(
            src_ref=q_ref.at[pl.ds(to * group, group)], dst_ref=qx.at[back(k)],
            send_sem=q_send.at[k], recv_sem=q_recv.at[back(k)],
            device_id=(to, c), device_id_type=MESH,
        )

    for k in range(1, nb):
        q_move(k).start()

    lane = lax.broadcasted_iota(jnp.int32, (size, LANES), 1) < size
    lane_x = lax.broadcasted_iota(jnp.int32, (EXTRA, LANES), 1) < size
    row_x = lax.broadcasted_iota(jnp.int32, (EXTRA, LANES), 0)
    ones = jnp.ones((EXTRA, tokens), jnp.bfloat16)

    nz, z_me, odd = nc // 2, c // 2, lax.rem(c, 2)
    partner = z_me * 2 + 1 - odd

    def pa_move(k):
        return pltpu.make_async_remote_copy(
            src_ref=part.at[k - 1], dst_ref=part_in.at[k - 1],
            send_sem=pa_send.at[k - 1], recv_sem=pa_recv.at[k - 1],
            device_id=(b, partner), device_id_type=MESH,
        )

    def rs_move(k):
        return pltpu.make_async_remote_copy(
            src_ref=both.at[k - 1], dst_ref=rs.at[k - 1],
            send_sem=rs_send.at[k - 1], recv_sem=rs_recv.at[k - 1],
            device_id=(b, lax.rem(z_me + k, nz) * 2 + odd), device_id_type=MESH,
        )

    def partial_sum(i, to):
        at = pl.multiple_of((i * nc + to) * LANES, LANES)
        feature = softplus(kt[pl.ds(at, LANES), :])
        left = jnp.concatenate([vt[pl.ds(at, LANES), :], ones], axis=0)
        s = lax.dot_general(left, feature, (((1,), (1,)), ((), ())), preferred_element_type=jnp.float32)
        return jnp.where(lane, s[:size], s[size : 2 * size]), s[2 * size :]

    def mass_of(block):
        return block[size : size + 1].astype(jnp.float32) + block[size + 1 : size + 2].astype(jnp.float32)

    k_copy.wait()
    v_copy.wait()

    def for_partner(k, carry):
        to = lax.rem(z_me + k, nz) * 2 + 1 - odd
        for i in range(ppd):
            state, mass = partial_sum(i, to)
            part[k - 1, i, :size, :] = state.astype(jnp.bfloat16)
            part[k - 1, i, size:, :] = split_mass(mass)

        @pl.when(k > 1)
        def _():
            pa_move(k - 1).start()

        return carry

    lax.fori_loop(1, nz + 1, for_partner, 0)
    pa_move(nz).start()

    def for_chip(k, carry):
        to = lax.rem(z_me + k, nz) * 2 + odd
        sums = [partial_sum(i, to) for i in range(ppd)]
        pa_move(k).wait_recv()
        for i, (state, mass) in enumerate(sums):
            block = part_in[k - 1, i]
            both[k - 1, i, :size, :] = (state + block[:size].astype(jnp.float32)).astype(jnp.bfloat16)
            both[k - 1, i, size:, :] = split_mass(mass + mass_of(block))

        @pl.when(k > 1)
        def _():
            rs_move(k - 1).start()

        return carry

    lax.fori_loop(1, nz + 1, for_chip, 0)

    for k in range(1, nz):
        rs_move(k).wait_recv()
    for i in range(ppd):
        blocks = [both[nz - 1, i]] + [rs[k - 1, i] for k in range(1, nz)]
        state = sum(x[:size].astype(jnp.float32) for x in blocks) / count
        mass = sum(mass_of(x) for x in blocks) / count
        own[i, :size, :] = state.astype(jnp.bfloat16)
        own[i, size:, :] = split_mass(jnp.broadcast_to(mass, (EXTRA, LANES)))

    def ag_move(i, k):
        p = i * nc + c
        g, slot = p // ppg, lax.rem(p, ppg)
        to = lax.rem(z_me + k, nz) * 2 + odd
        landing = b * ppg + slot
        remote = pltpu.make_async_remote_copy(
            src_ref=own.at[i], dst_ref=st.at[landing],
            send_sem=ag_send.at[i * nz + k], recv_sem=ag_recv.at[landing],
            device_id=(g, to), device_id_type=MESH,
        )
        local = pltpu.make_async_copy(own.at[i], st.at[landing], ag_recv.at[landing])
        return g, remote, local

    def fw_move(k, u):
        landing = ahead(k) * ppg + 2 * u + odd
        return pltpu.make_async_remote_copy(
            src_ref=st.at[landing], dst_ref=st.at[landing],
            send_sem=fw_send.at[landing], recv_sem=fw_recv.at[landing],
            device_id=(b, partner), device_id_type=MESH,
        )

    for k in range(nz):
        for i in range(ppd):
            g, remote, local = ag_move(i, k)
            if k > 0:
                remote.start()
            else:
                pl.when(g != b)(remote.start)
                pl.when(g == b)(local.start)

    for k in range(nb):
        if k == 0:
            q_copy.wait()
        else:
            q_move(back(k)).wait_recv()

        def featured(i, carry):
            at = pl.multiple_of(i * LANES, LANES)
            qx[k, pl.ds(at, LANES), :] = softplus(qx[k, pl.ds(at, LANES), :])
            return carry

        lax.fori_loop(0, ppg, featured, 0)

    def read(k, slot):
        at = ahead(k) * ppg + slot
        state = st[at, :size, :]
        mass = st[at, size:, :].astype(jnp.float32)
        hi, lo = mass[0:1], mass[1:2]
        low_half = jnp.where(lane_x, jnp.where(row_x == 0, hi, lo), 0.0)
        high_half = jnp.where(lane_x, 0.0, jnp.where(row_x == 2, hi, lo))
        m = jnp.where(row_x < 2, low_half, jnp.where(row_x < 4, high_half, 0.0)).astype(jnp.bfloat16)
        zero = jnp.zeros_like(state)
        left = jnp.concatenate([jnp.where(lane, state, zero), jnp.where(lane, zero, state), m], axis=0)
        column = pl.multiple_of(slot * LANES, LANES)
        y = lax.dot_general(
            left, qx[k, pl.ds(column, LANES), :], (((1,), (0,)), ((), ())),
            preferred_element_type=jnp.float32,
        )
        low = y[2 * size :]
        first = count**0.5 / (low[0:1] + low[1:2] + 0.001)
        second = count**0.5 / (low[2:3] + low[3:4] + 0.001)
        y = jnp.concatenate([y[:size] * first, y[size : 2 * size] * second], axis=0)
        mixed[k * tokens : (k + 1) * tokens, pl.ds(column, LANES)] = y.T.astype(jnp.bfloat16)

    for k in range(nb):
        for u in range(ppg // 2):
            at = ahead(k) * ppg + 2 * u + odd
            pltpu.make_async_copy(st.at[at], st.at[at], ag_recv.at[at]).wait()
            fw_move(k, u).start()
            read(k, 2 * u + odd)
    for k in range(nb):
        for u in range(ppg // 2):
            at = ahead(k) * ppg + 2 * u + 1 - odd
            pltpu.make_async_copy(st.at[at], st.at[at], fw_recv.at[at]).wait()
            read(k, 2 * u + 1 - odd)

    w_copy.wait()

    width = o_ref.shape[1] // chunks
    half = width // 2

    def place(axis, k):
        if axis == 0:
            return (y_me * nx + lax.rem(x_me + k, nx), c)
        return (lax.rem(y_me + k, ny) * nx + x_me, c)

    def offset(axis, k, other):
        return (other * nx + k) if axis == 0 else (k * nx + other)

    def first_move(j, h, k):
        n2 = ny if h == 0 else nx
        at = pl.ds((k - 1) * n2, n2)
        out_buf, in_buf, send, recv = stage1[h]
        return pltpu.make_async_remote_copy(
            src_ref=out_buf.at[j, at], dst_ref=in_buf.at[j, at],
            send_sem=send.at[j, k - 1], recv_sem=recv.at[j, k - 1],
            device_id=place(h, k), device_id_type=MESH,
        )

    def second_move(j, h, k):
        out_buf, in_buf, send, recv = stage2[h]
        return pltpu.make_async_remote_copy(
            src_ref=out_buf.at[j, k - 1], dst_ref=in_buf.at[j, k - 1],
            send_sem=send.at[j, k - 1], recv_sem=recv.at[j, k - 1],
            device_id=place(1 - h, k), device_id_type=MESH,
        )

    sizes = ((nx, ny), (ny, nx))

    def project(j, carry):
        at = pl.multiple_of(j * width, width)
        y = jnp.dot(mixed[...], wv[:, pl.ds(at, width)], preferred_element_type=jnp.float32)
        for h, (n1, n2) in enumerate(sizes):
            for k in range(n1):
                for other in range(n2):
                    r = offset(h, k, other) * tokens
                    piece = y[r : r + tokens, h * half : (h + 1) * half]
                    if k > 0:
                        stage1[h][0][j, (k - 1) * n2 + other] = piece.astype(jnp.bfloat16)
                    else:
                        mine[h][j, other] = piece
        for h, (n1, n2) in enumerate(sizes):
            for k in range(1, n1):
                first_move(j, h, k).start()
        return carry

    lax.fori_loop(0, chunks, project, 0)

    def relay(j, carry):
        for h, (n1, n2) in enumerate(sizes):
            for k in range(1, n1):
                first_move(j, h, k).wait_recv()
            for other in range(n2):
                y = mine[h][j, other]
                for k in range(1, n1):
                    y = y + stage1[h][1][j, (k - 1) * n2 + other].astype(jnp.float32)
                if other > 0:
                    stage2[h][0][j, other - 1] = y.astype(jnp.bfloat16)
                else:
                    mine[h][j, 0] = y
        for h, (n1, n2) in enumerate(sizes):
            for k in range(1, n2):
                second_move(j, h, k).start()
        return carry

    lax.fori_loop(0, chunks, relay, 0)

    def collect(j, carry):
        for h, (n1, n2) in enumerate(sizes):
            at = pl.multiple_of(j * width + h * half, half)
            y = mine[h][j, 0]
            for k in range(1, n2):
                second_move(j, h, k).wait_recv()
                y = y + stage2[h][1][j, k - 1].astype(jnp.float32)
            o_ref[:, pl.ds(at, half)] = y.astype(jnp.bfloat16)
        return carry

    lax.fori_loop(0, chunks, collect, 0)

    for k in range(1, nb):
        q_move(k).wait_send()

    for k in range(1, nz + 1):
        pa_move(k).wait_send()
    for k in range(1, nz):
        rs_move(k).wait_send()
    for k in range(nz):
        for i in range(ppd):
            g, remote, local = ag_move(i, k)
            if k > 0:
                remote.wait_send()
            else:
                pl.when(g != b)(remote.wait_send)
    for k in range(nb):
        for u in range(ppg // 2):
            fw_move(k, u).wait_send()

    def pr_end(j, carry):
        for h, (n1, n2) in enumerate(sizes):
            for k in range(1, n1):
                first_move(j, h, k).wait_send()
            for k in range(1, n2):
                second_move(j, h, k).wait_send()
        return carry

    lax.fori_loop(0, chunks, pr_end, 0)


def solution(mesh):
    nb, nc = mesh.shape["batch"], mesh.shape["ctx"]
    nx = next(n for n in range(math.isqrt(nb), 0, -1) if nb % n == 0)
    ny = nb // nx

    def shards(asked_for, offered, contents, out_weight):
        _, tokens, heads, size = asked_for.shape
        rows = heads * size
        depth, columns = out_weight.shape
        pairs = rows // LANES
        block = size + EXTRA
        width = CHUNK if columns % CHUNK == 0 else columns
        chunks = columns // width

        def flat(x):
            return x.transpose(0, 2, 3, 1).reshape(rows, tokens)

        bf16, f32 = jnp.bfloat16, jnp.float32
        dma = pltpu.SemaphoreType.DMA
        sizes = ((nx, ny), (ny, nx))

        def stage(blocks, moves):
            buffer = pltpu.VMEM((chunks, blocks, tokens, width // 2), bf16)
            return [buffer, buffer, dma((chunks, moves)), dma((chunks, moves))]

        out = pl.pallas_call(
            functools.partial(kernel, ny, nx, nc, size),
            out_shape=jax.ShapeDtypeStruct((tokens, columns), bf16),
            in_specs=[pl.BlockSpec(memory_space=pl.ANY)] * 4,
            out_specs=pl.BlockSpec(memory_space=pltpu.VMEM),
            scratch_shapes=[
                pltpu.VMEM((rows, tokens), bf16),
                pltpu.VMEM((rows, tokens), bf16),
                pltpu.VMEM((depth, columns), bf16),
                pltpu.VMEM((nb, rows // nb, tokens), bf16),
                pltpu.VMEM((nc // 2, pairs // nc, block, LANES), bf16),
                pltpu.VMEM((nc // 2, pairs // nc, block, LANES), bf16),
                pltpu.VMEM((nc // 2, pairs // nc, block, LANES), bf16),
                pltpu.VMEM((nc // 2, pairs // nc, block, LANES), bf16),
                pltpu.VMEM((pairs // nc, block, LANES), bf16),
                pltpu.VMEM((pairs, block, LANES), bf16),
                pltpu.VMEM((nb * tokens, rows // nb), bf16),
                [pltpu.VMEM((chunks, n2, tokens, width // 2), f32) for _, n2 in sizes],
                [stage((n1 - 1) * n2, n1 - 1) for n1, n2 in sizes],
                [stage(n2 - 1, n2 - 1) for _, n2 in sizes],
                dma((4,)),
                dma((nb,)),
                dma((nb,)),
                dma((nc // 2,)),
                dma((nc // 2,)),
                dma((nc // 2,)),
                dma((nc // 2,)),
                dma((pairs // 2,)),
                dma((pairs,)),
                dma((pairs,)),
                dma((pairs,)),
            ],
            compiler_params=pltpu.CompilerParams(
                collective_id=0, has_side_effects=True, vmem_limit_bytes=60 * 2**20
            ),
        )(flat(asked_for), flat(offered), flat(contents), out_weight)
        return out[None]

    in_specs = (
        P("batch", "ctx", None, None),
        P("batch", "ctx", None, None),
        P("batch", "ctx", None, None),
        P("batch", None),
    )
    return jax.shard_map(
        shards, mesh=mesh, in_specs=in_specs, out_specs=P("batch", "ctx", None), check_vma=False
    )
```

profile of v0, /device:TPU:0, one launch (start us, length us, event | category | flops | bytes accessed | tf_op | source)
XLA Modules:
  0.0 72.7 jit_solution(11110134602747093631)
XLA Ops:
  0.0 70.4 %shard_map.46 = bf16[128,4096]{1,0:T(8,128)(2,1)} custom-call(bf16[4096,128]{1,0:T(8,128)(2,1)} %bitcast.11, bf16[4096,128]{1,0:T(8,128)(2,1)} %bitcast.12, bf16[4096,128]{1,0:T(8,128)(2,1)} %bitcast.13, bf16[1024,4096]{1,0:T(8,128)(2,1)} %w_ref.1), custom_call_target="tpu_custom_call" | custom-call | tf_op jit(solution)/shard_map/pallas_call | solution.py:372
  70.4 2.3 %copy.6 = bf16[1,128,4096]{2,1,0:T(8,128)(2,1)} copy(bf16[1,128,4096]{2,1,0:T(8,128)(2,1)} %bitcast.10) | data formatting | bytes 2097152
where the time goes:
time: 72.9 us; the launch traced here: 72.7 us
  Pallas kernels  70.4 us (97%)
  local copies, waits for them, and re-layouts  2.29 us (3%)
    pallas_call x1, Pallas kernels, shards(): pl.pallas_call(functools.partial(kernel, ny, nx, nc, size), out_shape=jax...  70.4 us
    unnamed x1, local copies, waits for them, and re-layouts  2.29 us

commit v1 on v0

v1 whole, which is shorter than its diff:
```python
import functools
import math

import jax
import jax.numpy as jnp
from jax import lax
from jax.experimental import pallas as pl
from jax.experimental.pallas import tpu as pltpu
from jax.sharding import PartitionSpec as P

MESH = pl.DeviceIdType.MESH
LANES = 128
EXTRA = 8
CHUNK = 512


def softplus(x):
    x = x.astype(jnp.float32)
    return (jnp.maximum(x, 0.0) + jnp.log(1.0 + jnp.exp(-jnp.abs(x)))).astype(jnp.bfloat16)


def kernel(
    ny, nx, nc, size, grid, q_ref, k_ref, v_ref, w_ref, o_ref,
    kt, vt, wv, qx, ft, part, part_in, both, rs, own, st, mixed, mine, stage1, stage2,
    local_sem, q_send, q_recv, pa_send, pa_recv, rs_send, rs_recv,
    ag_send, ag_recv, fw_send, fw_recv,
):
    b, c = lax.axis_index("batch"), lax.axis_index("ctx")
    nb = ny * nx
    rows, tokens = k_ref.shape
    pairs = rows // LANES
    ppg = pairs // nb
    group = rows // nb
    messages, held, spread = grid
    blocks = ppg // held
    base = held * size
    total = nb * nc
    me = b * nc + c
    count = tokens * nc
    chunks = mine[0].shape[0]
    nz, z_me, odd = nc // 2, c // 2, lax.rem(c, 2)
    partner = z_me * 2 + 1 - odd
    y_me, x_me = b // nx, lax.rem(b, nx)

    k_copy = pltpu.make_async_copy(k_ref, kt, local_sem.at[0])
    v_copy = pltpu.make_async_copy(v_ref, vt, local_sem.at[1])
    q_copy = pltpu.make_async_copy(q_ref.at[pl.ds(b * group, group)], qx.at[0], local_sem.at[2])
    w_copy = pltpu.make_async_copy(w_ref, wv, local_sem.at[3])
    k_copy.start()
    v_copy.start()
    q_copy.start()
    w_copy.start()

    barrier = pltpu.get_barrier_semaphore()

    def greet(i, carry):
        d = lax.rem(me + i, total)
        pl.semaphore_signal(barrier, inc=1, device_id=(d // nc, lax.rem(d, nc)), device_id_type=MESH)
        return carry

    lax.fori_loop(1, total, greet, 0)

    def ahead(k):
        return lax.rem(y_me + k // nx, ny) * nx + lax.rem(x_me + k % nx, nx)

    def back(k):
        return (ny - k // nx) % ny * nx + (nx - k % nx) % nx

    def q_move(k):
        to = ahead(k)
        return pltpu.make_async_remote_copy(
            src_ref=q_ref.at[pl.ds(to * group, group)], dst_ref=qx.at[back(k)],
            send_sem=q_send.at[k], recv_sem=q_recv.at[back(k)],
            device_id=(to, c), device_id_type=MESH,
        )

    lane = lax.broadcasted_iota(jnp.int32, (size, LANES), 1) < size
    row_x = lax.broadcasted_iota(jnp.int32, (EXTRA, LANES), 0)
    ones = jnp.ones((2 * EXTRA, tokens), jnp.bfloat16)

    def first_pair(j, owner):
        if spread:
            return (lax.rem(owner, 2) * messages + j) * ppg + owner // 2 * held
        return j * nc + owner

    def pa_move(j, k):
        return pltpu.make_async_remote_copy(
            src_ref=part.at[j, k - 1], dst_ref=part_in.at[j, k - 1],
            send_sem=pa_send.at[j, k - 1], recv_sem=pa_recv.at[j, k - 1],
            device_id=(b, partner), device_id_type=MESH,
        )

    def rs_move(j, k):
        return pltpu.make_async_remote_copy(
            src_ref=both.at[j, k - 1], dst_ref=rs.at[j, k - 1],
            send_sem=rs_send.at[j, k - 1], recv_sem=rs_recv.at[j, k - 1],
            device_id=(b, lax.rem(z_me + k, nz) * 2 + odd), device_id_type=MESH,
        )

    def partial_sum(p):
        at = pl.multiple_of(p * LANES, LANES)
        feature = softplus(kt[pl.ds(at, LANES), :])
        left = jnp.concatenate([vt[pl.ds(at, LANES), :], ones], axis=0)
        s = lax.dot_general(left, feature, (((1,), (1,)), ((), ())), preferred_element_type=jnp.float32)
        return jnp.where(lane, s[:size], s[size : 2 * size]), s[2 * size : 2 * size + EXTRA]

    def split_mass(masses):
        packed = jnp.zeros((EXTRA, LANES), jnp.float32)
        for t, m in enumerate(masses):
            high = m.astype(jnp.bfloat16).astype(jnp.float32)
            packed = jnp.where(row_x == 2 * t, high, jnp.where(row_x == 2 * t + 1, m - high, packed))
        return packed.astype(jnp.bfloat16)

    def states_of(block):
        return [block[t * size : (t + 1) * size].astype(jnp.float32) for t in range(held)]

    def masses_of(block):
        extra = block[base:].astype(jnp.float32)
        return [extra[2 * t : 2 * t + 1] + extra[2 * t + 1 : 2 * t + 2] for t in range(held)]

    k_copy.wait()
    v_copy.wait()

    for j in range(messages):

        def for_partner(k, carry):
            owner = lax.rem(z_me + k, nz) * 2 + 1 - odd
            sums = [partial_sum(first_pair(j, owner) + t) for t in range(held)]
            for t, (state, _) in enumerate(sums):
                part[j, k - 1, t * size : (t + 1) * size, :] = state.astype(jnp.bfloat16)
            part[j, k - 1, base:, :] = split_mass([m for _, m in sums])
            return carry

        lax.fori_loop(1, nz + 1, for_partner, 0)

    pl.semaphore_wait(barrier, total - 1)

    for j in range(messages):
        for k in range(1, nz + 1):
            pa_move(j, k).start()
    for k in range(1, nb):
        q_move(k).start()

    for j in range(messages):

        def for_chip(k, carry):
            owner = lax.rem(z_me + k, nz) * 2 + odd
            sums = [partial_sum(first_pair(j, owner) + t) for t in range(held)]
            pa_move(j, k).wait_recv()
            block = part_in[j, k - 1]
            for t, ((state, _), other) in enumerate(zip(sums, states_of(block))):
                both[j, k - 1, t * size : (t + 1) * size, :] = (state + other).astype(jnp.bfloat16)
            both[j, k - 1, base:, :] = split_mass([m + o for (_, m), o in zip(sums, masses_of(block))])

            @pl.when(k < nz)
            def _():
                rs_move(j, k).start()

            return carry

        lax.fori_loop(1, nz + 1, for_chip, 0)

    def features(k):
        def featured(i, carry):
            at = pl.multiple_of(i * LANES, LANES)
            ft[k, i] = softplus(qx[k, pl.ds(at, LANES), :]).T
            return carry

        lax.fori_loop(0, ppg, featured, 0)

    q_copy.wait()
    features(0)

    def ag_move(j, k):
        p = first_pair(j, c)
        g = p // ppg
        block = lax.rem(p, ppg) // held
        side = lax.rem(block, 2)
        to = lax.rem(z_me + k, nz) * 2 + side
        landing = b * blocks + block
        remote = pltpu.make_async_remote_copy(
            src_ref=own.at[j], dst_ref=st.at[landing],
            send_sem=ag_send.at[j * nz + k], recv_sem=ag_recv.at[landing],
            device_id=(g, to), device_id_type=MESH,
        )
        local = pltpu.make_async_copy(own.at[j], st.at[landing], ag_recv.at[landing])
        here = jnp.logical_and(g == b, side == odd)
        return here, remote, local

    for j in range(messages):
        for k in range(1, nz):
            rs_move(j, k).wait_recv()
        parts = [both[j, nz - 1]] + [rs[j, k - 1] for k in range(1, nz)]
        states = [sum(x) / count for x in zip(*[states_of(p) for p in parts])]
        masses = [sum(x) / count for x in zip(*[masses_of(p) for p in parts])]
        for t, state in enumerate(states):
            own[j, t * size : (t + 1) * size, :] = state.astype(jnp.bfloat16)
        own[j, base:, :] = split_mass([jnp.broadcast_to(m, (EXTRA, LANES)) for m in masses])
        for k in range(1, nz):
            ag_move(j, k)[1].start()
        here, remote, local = ag_move(j, 0)
        pl.when(jnp.logical_not(here))(remote.start)
        pl.when(here)(local.start)

    for k in range(1, nb):
        q_move(back(k)).wait_recv()
        features(k)

    def fw_move(k, u):
        landing = ahead(k) * blocks + 2 * u + odd
        return pltpu.make_async_remote_copy(
            src_ref=st.at[landing], dst_ref=st.at[landing],
            send_sem=fw_send.at[landing], recv_sem=fw_recv.at[landing],
            device_id=(b, partner), device_id_type=MESH,
        )

    def read(k, block):
        at = ahead(k) * blocks + block
        for t in range(held):
            state = st[at, t * size : (t + 1) * size, :]
            mass = st[at, base:, :].astype(jnp.float32)
            mass = jnp.broadcast_to(mass[2 * t : 2 * t + 1], (size, LANES)).astype(jnp.bfloat16)
            zero = jnp.zeros_like(state)
            right = jnp.concatenate(
                [jnp.where(lane, x, zero) if low else jnp.where(lane, zero, x)
                 for x in (state, mass) for low in (True, False)], axis=0,
            )
            slot = block * held + t
            y = lax.dot_general(
                ft[k, slot], right, (((1,), (1,)), ((), ())), preferred_element_type=jnp.float32
            )
            y = y[:, :LANES] * (count**0.5 / (y[:, LANES:] + 0.001))
            column = pl.multiple_of(slot * LANES, LANES)
            mixed[k * tokens : (k + 1) * tokens, pl.ds(column, LANES)] = y.astype(jnp.bfloat16)

    for u in range(blocks // 2):
        for k in range(nb):
            at = ahead(k) * blocks + 2 * u + odd
            pltpu.make_async_copy(st.at[at], st.at[at], ag_recv.at[at]).wait()
            fw_move(k, u).start()
            read(k, 2 * u + odd)
    for u in range(blocks // 2):
        for k in range(nb):
            at = ahead(k) * blocks + 2 * u + 1 - odd
            pltpu.make_async_copy(st.at[at], st.at[at], fw_recv.at[at]).wait()
            read(k, 2 * u + 1 - odd)

    w_copy.wait()

    width = o_ref.shape[1] // chunks
    half = width // 2

    def place(axis, k):
        if axis == 0:
            return (y_me * nx + lax.rem(x_me + k, nx), c)
        return (lax.rem(y_me + k, ny) * nx + x_me, c)

    def offset(axis, k, other):
        return (other * nx + k) if axis == 0 else (k * nx + other)

    def first_move(j, h, k):
        n2 = ny if h == 0 else nx
        at = pl.ds((k - 1) * n2, n2)
        out_buf, in_buf, send, recv = stage1[h]
        return pltpu.make_async_remote_copy(
            src_ref=out_buf.at[j, at], dst_ref=in_buf.at[j, at],
            send_sem=send.at[j, k - 1], recv_sem=recv.at[j, k - 1],
            device_id=place(h, k), device_id_type=MESH,
        )

    def second_move(j, h, k):
        out_buf, in_buf, send, recv = stage2[h]
        return pltpu.make_async_remote_copy(
            src_ref=out_buf.at[j, k - 1], dst_ref=in_buf.at[j, k - 1],
            send_sem=send.at[j, k - 1], recv_sem=recv.at[j, k - 1],
            device_id=place(1 - h, k), device_id_type=MESH,
        )

    sizes = ((nx, ny), (ny, nx))

    def project(j, carry):
        at = pl.multiple_of(j * width, width)
        y = jnp.dot(mixed[...], wv[:, pl.ds(at, width)], preferred_element_type=jnp.float32)
        for h, (n1, n2) in enumerate(sizes):
            for k in range(n1):
                for other in range(n2):
                    r = offset(h, k, other) * tokens
                    piece = y[r : r + tokens, h * half : (h + 1) * half]
                    if k > 0:
                        stage1[h][0][j, (k - 1) * n2 + other] = piece.astype(jnp.bfloat16)
                    else:
                        mine[h][j, other] = piece
        for h, (n1, n2) in enumerate(sizes):
            for k in range(1, n1):
                first_move(j, h, k).start()
        return carry

    lax.fori_loop(0, chunks, project, 0)

    def relay(j, carry):
        for h, (n1, n2) in enumerate(sizes):
            for k in range(1, n1):
                first_move(j, h, k).wait_recv()
            for other in range(n2):
                y = mine[h][j, other]
                for k in range(1, n1):
                    y = y + stage1[h][1][j, (k - 1) * n2 + other].astype(jnp.float32)
                if other > 0:
                    stage2[h][0][j, other - 1] = y.astype(jnp.bfloat16)
                else:
                    mine[h][j, 0] = y
        for h, (n1, n2) in enumerate(sizes):
            for k in range(1, n2):
                second_move(j, h, k).start()
        return carry

    lax.fori_loop(0, chunks, relay, 0)

    def collect(j, carry):
        for h, (n1, n2) in enumerate(sizes):
            at = pl.multiple_of(j * width + h * half, half)
            y = mine[h][j, 0]
            for k in range(1, n2):
                second_move(j, h, k).wait_recv()
                y = y + stage2[h][1][j, k - 1].astype(jnp.float32)
            o_ref[:, pl.ds(at, half)] = y.astype(jnp.bfloat16)
        return carry

    lax.fori_loop(0, chunks, collect, 0)

    for k in range(1, nb):
        q_move(k).wait_send()

    for j in range(messages):
        for k in range(1, nz + 1):
            pa_move(j, k).wait_send()
        for k in range(1, nz):
            rs_move(j, k).wait_send()
            ag_move(j, k)[1].wait_send()
        here, remote, _ = ag_move(j, 0)
        pl.when(jnp.logical_not(here))(remote.wait_send)
    for k in range(nb):
        for u in range(blocks // 2):
            fw_move(k, u).wait_send()

    def pr_end(j, carry):
        for h, (n1, n2) in enumerate(sizes):
            for k in range(1, n1):
                first_move(j, h, k).wait_send()
            for k in range(1, n2):
                second_move(j, h, k).wait_send()
        return carry

    lax.fori_loop(0, chunks, pr_end, 0)


def solution(mesh):
    nb, nc = mesh.shape["batch"], mesh.shape["ctx"]
    nx = next(n for n in range(math.isqrt(nb), 0, -1) if nb % n == 0)
    ny = nb // nx

    def shards(asked_for, offered, contents, out_weight):
        _, tokens, heads, size = asked_for.shape
        rows = heads * size
        depth, columns = out_weight.shape
        pairs = rows // LANES
        width = CHUNK if columns % CHUNK == 0 else columns
        chunks = columns // width

        def flat(x):
            return x.transpose(0, 2, 3, 1).reshape(rows, tokens)

        bf16, f32 = jnp.bfloat16, jnp.float32
        dma = pltpu.SemaphoreType.DMA
        sizes = ((nx, ny), (ny, nx))

        def stage(blocks, moves):
            buffer = pltpu.VMEM((chunks, blocks, tokens, width // 2), bf16)
            return [buffer, buffer, dma((chunks, moves)), dma((chunks, moves))]

        half_pairs, ppg = nc // 2, pairs // nb
        spread = nb % 2 == 0 and ppg % half_pairs == 0 and ppg >= half_pairs
        held = ppg // half_pairs if spread else 1
        messages = pairs // nc // held
        high = held * size + EXTRA
        hops = pltpu.VMEM((messages, nc // 2, high, LANES), bf16)
        scratch = [
            pltpu.VMEM((rows, tokens), bf16),
            pltpu.VMEM((rows, tokens), bf16),
            pltpu.VMEM((depth, columns), bf16),
            pltpu.VMEM((nb, rows // nb, tokens), bf16),
            pltpu.VMEM((nb, ppg, tokens, LANES), bf16),
            hops,
            hops,
            hops,
            hops,
            pltpu.VMEM((messages, high, LANES), bf16),
            pltpu.VMEM((pairs // held, high, LANES), bf16),
            pltpu.VMEM((nb * tokens, rows // nb), bf16),
            [pltpu.VMEM((chunks, n2, tokens, width // 2), f32) for _, n2 in sizes],
            [stage((n1 - 1) * n2, n1 - 1) for n1, n2 in sizes],
            [stage(n2 - 1, n2 - 1) for _, n2 in sizes],
            dma((4,)),
            dma((nb,)),
            dma((nb,)),
            dma((messages, nc // 2)),
            dma((messages, nc // 2)),
            dma((messages, nc // 2)),
            dma((messages, nc // 2)),
            dma((messages * nc // 2,)),
            dma((pairs // held,)),
            dma((pairs // held,)),
            dma((pairs // held,)),
        ]
        buffers = [x for x in jax.tree.leaves(scratch, is_leaf=lambda x: hasattr(x, "shape")) if x.dtype in (bf16, f32)]
        used = sum(math.prod(x.shape) * jnp.dtype(x.dtype).itemsize for x in buffers)
        limit = used + 4 * tokens * columns + 3 * 2**20

        out = pl.pallas_call(
            functools.partial(kernel, ny, nx, nc, size, (messages, held, spread)),
            out_shape=jax.ShapeDtypeStruct((tokens, columns), bf16),
            in_specs=[pl.BlockSpec(memory_space=pl.ANY)] * 4,
            out_specs=pl.BlockSpec(memory_space=pltpu.VMEM),
            scratch_shapes=scratch,
            compiler_params=pltpu.CompilerParams(
                collective_id=0, has_side_effects=True, vmem_limit_bytes=max(limit, 52 * 2**20)
            ),
        )(flat(asked_for), flat(offered), flat(contents), out_weight)
        return out[None]

    in_specs = (
        P("batch", "ctx", None, None),
        P("batch", "ctx", None, None),
        P("batch", "ctx", None, None),
        P("batch", None),
    )
    return jax.shard_map(
        shards, mesh=mesh, in_specs=in_specs, out_specs=P("batch", "ctx", None), check_vma=False
    )
```

time: 72.9 us -> 66.7 us (0.915)
  Pallas kernels: 70.4 us -> 65.6 us
  local copies, waits for them, and re-layouts: 2.29 us -> 0.97 us
    pallas_call x1, Pallas kernels: 70.4 us -> 65.6 us  [shards(): pl.pallas_call(functools.partial(kernel, ny, nx, nc, size, (messages, hel...]
    unnamed x1, local copies, waits for them, and re-layouts: 2.29 us -> 0.97 us
where the time goes in v1:
time: 66.7 us; the launch traced here: 66.6 us
  Pallas kernels  65.6 us (98%)
  local copies, waits for them, and re-layouts  0.97 us (1%)
    pallas_call x1, Pallas kernels, shards(): pl.pallas_call(functools.partial(kernel, ny, nx, nc, size, (messages, hel...  65.6 us

profile of v1, /device:TPU:0, one launch (start us, length us, event | category | flops | bytes accessed | tf_op | source)
XLA Modules:
  0.0 66.6 jit_solution(16529486846140072917)
XLA Ops:
  0.0 65.6 %shard_map.46 = bf16[128,4096]{1,0:T(8,128)(2,1)S(1)} custom-call(bf16[4096,128]{1,0:T(8,128)(2,1)} %bitcast.11, bf16[4096,128]{1,0:T(8,128)(2,1)} %bitcast.12, bf16[4096,128]{1,0:T(8,128)(2,1)} %bitcast.13, bf16[1024,4096]{1,0:T(8,128)(2,1)} %w_ref.1), custom_call_target="tpu_custom_call" | custom-call | tf_op jit(solution)/shard_map/pallas_call | solution.py:419
  65.6 1.0 %copy.6 = bf16[1,128,4096]{2,1,0:T(8,128)(2,1)} copy(bf16[1,128,4096]{2,1,0:T(8,128)(2,1)S(1)} %bitcast.10) | data formatting | bytes 2097152

commit v2 on v1

--- a/solution.py
+++ b/solution.py
@@ -66,6 +66,10 @@
     def back(k):
         return (ny - k // nx) % ny * nx + (nx - k % nx) % nx
 
+    near = [k for k in range(1, nb) if k < nx or k % nx == 0]
+    far = [k for k in range(1, nb) if k not in near]
+    order = near + far + [0]
+
     def q_move(k):
         to = ahead(k)
         return pltpu.make_async_remote_copy(
@@ -80,7 +84,8 @@
 
     def first_pair(j, owner):
         if spread:
-            return (lax.rem(owner, 2) * messages + j) * ppg + owner // 2 * held
+            even, uneven = order[2 * j], order[2 * j + 1]
+            return jnp.where(lax.rem(owner, 2) == 0, ahead(even), ahead(uneven)) * ppg + owner // 2 * held
         return j * nc + owner
 
     def pa_move(j, k):
@@ -138,7 +143,7 @@
     for j in range(messages):
         for k in range(1, nz + 1):
             pa_move(j, k).start()
-    for k in range(1, nb):
+    for k in near:
         q_move(k).start()
 
     for j in range(messages):
@@ -201,10 +206,12 @@
         here, remote, local = ag_move(j, 0)
         pl.when(jnp.logical_not(here))(remote.start)
         pl.when(here)(local.start)
-
-    for k in range(1, nb):
-        q_move(back(k)).wait_recv()
-        features(k)
+        if j == 0:
+            for k in far:
+                q_move(k).start()
+            for k in near:
+                q_move(back(k)).wait_recv()
+                features(k)
 
     def fw_move(k, u):
         landing = ahead(k) * blocks + 2 * u + odd
@@ -233,17 +240,20 @@
             column = pl.multiple_of(slot * LANES, LANES)
             mixed[k * tokens : (k + 1) * tokens, pl.ds(column, LANES)] = y.astype(jnp.bfloat16)
 
-    for u in range(blocks // 2):
-        for k in range(nb):
-            at = ahead(k) * blocks + 2 * u + odd
-            pltpu.make_async_copy(st.at[at], st.at[at], ag_recv.at[at]).wait()
-            fw_move(k, u).start()
-            read(k, 2 * u + odd)
-    for u in range(blocks // 2):
-        for k in range(nb):
-            at = ahead(k) * blocks + 2 * u + 1 - odd
-            pltpu.make_async_copy(st.at[at], st.at[at], fw_recv.at[at]).wait()
-            read(k, 2 * u + 1 - odd)
+    def read_all(sequences):
+        for u in range(blocks // 2):
+            for k in sequences:
+                at = ahead(k) * blocks + 2 * u + odd
+                pltpu.make_async_copy(st.at[at], st.at[at], ag_recv.at[at]).wait()
+                fw_move(k, u).start()
+                read(k, 2 * u + odd)
+        for u in range(blocks // 2):
+            for k in sequences:
+                at = ahead(k) * blocks + 2 * u + 1 - odd
+                pltpu.make_async_copy(st.at[at], st.at[at], fw_recv.at[at]).wait()
+                read(k, 2 * u + 1 - odd)
+
+    read_all(near)
 
     w_copy.wait()
 
@@ -258,13 +268,12 @@
     def offset(axis, k, other):
         return (other * nx + k) if axis == 0 else (k * nx + other)
 
-    def first_move(j, h, k):
-        n2 = ny if h == 0 else nx
-        at = pl.ds((k - 1) * n2, n2)
+    def first_move(j, h, k, other):
+        at = (k - 1) * (ny if h == 0 else nx) + other
         out_buf, in_buf, send, recv = stage1[h]
         return pltpu.make_async_remote_copy(
             src_ref=out_buf.at[j, at], dst_ref=in_buf.at[j, at],
-            send_sem=send.at[j, k - 1], recv_sem=recv.at[j, k - 1],
+            send_sem=send.at[j, at], recv_sem=recv.at[j, at],
             device_id=place(h, k), device_id_type=MESH,
         )
 
@@ -278,37 +287,46 @@
 
     sizes = ((nx, ny), (ny, nx))
 
-    def project(j, carry):
-        at = pl.multiple_of(j * width, width)
-        y = jnp.dot(mixed[...], wv[:, pl.ds(at, width)], preferred_element_type=jnp.float32)
+    def projected(j, h, k, other):
+        r = offset(h, k, other) * tokens
+        at = pl.multiple_of(j * width + h * half, half)
+        return jnp.dot(mixed[r : r + tokens, :], wv[:, pl.ds(at, half)], preferred_element_type=jnp.float32)
+
+    def send_rows(others):
+        def project(j, carry):
+            for h, (n1, n2) in enumerate(sizes):
+                for k in range(1, n1):
+                    for other in others(n2):
+                        y = projected(j, h, k, other)
+                        stage1[h][0][j, (k - 1) * n2 + other] = y.astype(jnp.bfloat16)
+                        first_move(j, h, k, other).start()
+            return carry
+
+        lax.fori_loop(0, chunks, project, 0)
+
+    def keep_rows(j, carry):
         for h, (n1, n2) in enumerate(sizes):
-            for k in range(n1):
-                for other in range(n2):
-                    r = offset(h, k, other) * tokens
-                    piece = y[r : r + tokens, h * half : (h + 1) * half]
-                    if k > 0:
-                        stage1[h][0][j, (k - 1) * n2 + other] = piece.astype(jnp.bfloat16)
-                    else:
-                        mine[h][j, other] = piece
-        for h, (n1, n2) in enumerate(sizes):
-            for k in range(1, n1):
-                first_move(j, h, k).start()
+            for other in range(n2):
+                mine[h][j, other] = projected(j, h, 0, other)
         return carry
 
-    lax.fori_loop(0, chunks, project, 0)
+    send_rows(lambda n2: [0])
+    for k in far:
+        q_move(back(k)).wait_recv()
+        features(k)
+    read_all(far)
+    send_rows(lambda n2: range(1, n2))
+    read_all([0])
+    lax.fori_loop(0, chunks, keep_rows, 0)
 
     def relay(j, carry):
         for h, (n1, n2) in enumerate(sizes):
-            for k in range(1, n1):
-                first_move(j, h, k).wait_recv()
-            for other in range(n2):
+            for other in range(1, n2):
                 y = mine[h][j, other]
                 for k in range(1, n1):
+                    first_move(j, h, k, other).wait_recv()
                     y = y + stage1[h][1][j, (k - 1) * n2 + other].astype(jnp.float32)
-                if other > 0:
-                    stage2[h][0][j, other - 1] = y.astype(jnp.bfloat16)
-                else:
-                    mine[h][j, 0] = y
+                stage2[h][0][j, other - 1] = y.astype(jnp.bfloat16)
         for h, (n1, n2) in enumerate(sizes):
             for k in range(1, n2):
                 second_move(j, h, k).start()
@@ -320,6 +338,9 @@
         for h, (n1, n2) in enumerate(sizes):
             at = pl.multiple_of(j * width + h * half, half)
             y = mine[h][j, 0]
+            for k in range(1, n1):
+                first_move(j, h, k, 0).wait_recv()
+                y = y + stage1[h][1][j, (k - 1) * n2].astype(jnp.float32)
             for k in range(1, n2):
                 second_move(j, h, k).wait_recv()
                 y = y + stage2[h][1][j, k - 1].astype(jnp.float32)
@@ -346,7 +367,8 @@
     def pr_end(j, carry):
         for h, (n1, n2) in enumerate(sizes):
             for k in range(1, n1):
-                first_move(j, h, k).wait_send()
+                for other in range(n2):
+                    first_move(j, h, k, other).wait_send()
             for k in range(1, n2):
                 second_move(j, h, k).wait_send()
         return carry
@@ -398,7 +420,7 @@
             pltpu.VMEM((pairs // held, high, LANES), bf16),
             pltpu.VMEM((nb * tokens, rows // nb), bf16),
             [pltpu.VMEM((chunks, n2, tokens, width // 2), f32) for _, n2 in sizes],
-            [stage((n1 - 1) * n2, n1 - 1) for n1, n2 in sizes],
+            [stage((n1 - 1) * n2, (n1 - 1) * n2) for n1, n2 in sizes],
             [stage(n2 - 1, n2 - 1) for _, n2 in sizes],
             dma((4,)),
             dma((nb,)),

time: 66.7 us -> 61 us (0.915)
  Pallas kernels: 65.6 us -> 59.8 us
    pallas_call x1, Pallas kernels: 65.6 us -> 59.8 us  [shards(): pl.pallas_call(functools.partial(kernel, ny, nx, nc, size, (messages, hel...]
where the time goes in v2:
time: 61 us; the launch traced here: 60.8 us
  Pallas kernels  59.8 us (98%)
  local copies, waits for them, and re-layouts  0.97 us (2%)
    pallas_call x1, Pallas kernels, shards(): pl.pallas_call(functools.partial(kernel, ny, nx, nc, size, (messages, hel...  59.8 us

profile of v2, /device:TPU:0, one launch (start us, length us, event | category | flops | bytes accessed | tf_op | source)
XLA Modules:
  0.0 60.8 jit_solution(17452864616894400501)
XLA Ops:
  0.0 59.8 %shard_map.46 = bf16[128,4096]{1,0:T(8,128)(2,1)S(1)} custom-call(bf16[4096,128]{1,0:T(8,128)(2,1)} %bitcast.11, bf16[4096,128]{1,0:T(8,128)(2,1)} %bitcast.12, bf16[4096,128]{1,0:T(8,128)(2,1)} %bitcast.13, bf16[1024,4096]{1,0:T(8,128)(2,1)} %w_ref.1), custom_call_target="tpu_custom_call" | custom-call | tf_op jit(solution)/shard_map/pallas_call | solution.py:441
  59.9 1.0 %copy.6 = bf16[1,128,4096]{2,1,0:T(8,128)(2,1)} copy(bf16[1,128,4096]{2,1,0:T(8,128)(2,1)S(1)} %bitcast.10) | data formatting | bytes 2097152

commit v3 on v2

--- a/solution.py
+++ b/solution.py
@@ -12,6 +12,8 @@
 LANES = 128
 EXTRA = 8
 CHUNK = 512
+PIECES = 4
+EARLY = 0
 
 
 def softplus(x):
@@ -22,7 +24,7 @@
 def kernel(
     ny, nx, nc, size, grid, q_ref, k_ref, v_ref, w_ref, o_ref,
     kt, vt, wv, qx, ft, part, part_in, both, rs, own, st, mixed, mine, stage1, stage2,
-    local_sem, q_send, q_recv, pa_send, pa_recv, rs_send, rs_recv,
+    local_sem, load_sem, q_send, q_recv, pa_send, pa_recv, rs_send, rs_recv,
     ag_send, ag_recv, fw_send, fw_recv,
 ):
     b, c = lax.axis_index("batch"), lax.axis_index("ctx")
@@ -30,36 +32,16 @@
     rows, tokens = k_ref.shape
     pairs = rows // LANES
     ppg = pairs // nb
-    group = rows // nb
-    messages, held, spread = grid
+    share = rows // nb
+    messages, held, rounds, spread = grid
     blocks = ppg // held
     base = held * size
-    total = nb * nc
-    me = b * nc + c
     count = tokens * nc
     chunks = mine[0].shape[0]
     nz, z_me, odd = nc // 2, c // 2, lax.rem(c, 2)
     partner = z_me * 2 + 1 - odd
     y_me, x_me = b // nx, lax.rem(b, nx)
 
-    k_copy = pltpu.make_async_copy(k_ref, kt, local_sem.at[0])
-    v_copy = pltpu.make_async_copy(v_ref, vt, local_sem.at[1])
-    q_copy = pltpu.make_async_copy(q_ref.at[pl.ds(b * group, group)], qx.at[0], local_sem.at[2])
-    w_copy = pltpu.make_async_copy(w_ref, wv, local_sem.at[3])
-    k_copy.start()
-    v_copy.start()
-    q_copy.start()
-    w_copy.start()
-
-    barrier = pltpu.get_barrier_semaphore()
-
-    def greet(i, carry):
-        d = lax.rem(me + i, total)
-        pl.semaphore_signal(barrier, inc=1, device_id=(d // nc, lax.rem(d, nc)), device_id_type=MESH)
-        return carry
-
-    lax.fori_loop(1, total, greet, 0)
-
     def ahead(k):
         return lax.rem(y_me + k // nx, ny) * nx + lax.rem(x_me + k % nx, nx)
 
@@ -70,11 +52,40 @@
     far = [k for k in range(1, nb) if k not in near]
     order = near + far + [0]
 
-    def q_move(k):
+    def load(i):
+        at = pl.ds(ahead(order[i]) * share, share)
+        return [
+            pltpu.make_async_copy(ref.at[at], buffer.at[at], load_sem.at[n, i])
+            for n, (ref, buffer) in enumerate(((k_ref, kt), (v_ref, vt)))
+        ]
+
+    q_copy = pltpu.make_async_copy(q_ref.at[pl.ds(b * share, share)], qx.at[0], local_sem.at[2])
+    w_copy = pltpu.make_async_copy(w_ref, wv, local_sem.at[3])
+    for i in range(nb):
+        for copy in load(i):
+            copy.start()
+    q_copy.start()
+    w_copy.start()
+
+    barrier = pltpu.get_barrier_semaphore()
+
+    def greet(device):
+        pl.semaphore_signal(barrier, inc=1, device_id=device, device_id_type=MESH)
+
+    greet((b, partner))
+    for k in range(1, nb):
+        greet((lax.rem(b + k, nb), c))
+    for k in range(1, nz):
+        greet((b, lax.rem(c + 2 * k, nc)))
+
+    piece = share // PIECES
+
+    def q_move(k, n):
         to = ahead(k)
+        at = pl.ds(pl.multiple_of(to * share + n * piece, piece), piece)
         return pltpu.make_async_remote_copy(
-            src_ref=q_ref.at[pl.ds(to * group, group)], dst_ref=qx.at[back(k)],
-            send_sem=q_send.at[k], recv_sem=q_recv.at[back(k)],
+            src_ref=q_ref.at[at], dst_ref=qx.at[back(k), pl.ds(n * piece, piece)],
+            send_sem=q_send.at[k, n], recv_sem=q_recv.at[back(k), n],
             device_id=(to, c), device_id_type=MESH,
         )
 
@@ -84,9 +95,13 @@
 
     def first_pair(j, owner):
         if spread:
-            even, uneven = order[2 * j], order[2 * j + 1]
-            return jnp.where(lax.rem(owner, 2) == 0, ahead(even), ahead(uneven)) * ppg + owner // 2 * held
+            even, uneven = order[j // rounds * 2], order[j // rounds * 2 + 1]
+            group = jnp.where(lax.rem(owner, 2) == 0, ahead(even), ahead(uneven))
+            return group * ppg + (owner // 2 * rounds + j % rounds) * held
         return j * nc + owner
+
+    urgent = min(rounds, messages) if spread else 1
+    late = 1 if messages > urgent and rounds > 1 else 0
 
     def pa_move(j, k):
         return pltpu.make_async_remote_copy(
@@ -123,55 +138,76 @@
         extra = block[base:].astype(jnp.float32)
         return [extra[2 * t : 2 * t + 1] + extra[2 * t + 1 : 2 * t + 2] for t in range(held)]
 
-    k_copy.wait()
-    v_copy.wait()
-
-    for j in range(messages):
-
+    batches = [range(j, min(j + rounds, messages)) for j in range(0, messages, rounds)]
+
+    def sum_for_partner(batch):
         def for_partner(k, carry):
             owner = lax.rem(z_me + k, nz) * 2 + 1 - odd
-            sums = [partial_sum(first_pair(j, owner) + t) for t in range(held)]
-            for t, (state, _) in enumerate(sums):
-                part[j, k - 1, t * size : (t + 1) * size, :] = state.astype(jnp.bfloat16)
-            part[j, k - 1, base:, :] = split_mass([m for _, m in sums])
+            for j in batch:
+                sums = [partial_sum(first_pair(j, owner) + t) for t in range(held)]
+                for t, (state, _) in enumerate(sums):
+                    part[j, k - 1, t * size : (t + 1) * size, :] = state.astype(jnp.bfloat16)
+                part[j, k - 1, base:, :] = split_mass([m for _, m in sums])
             return carry
 
-        lax.fori_loop(1, nz + 1, for_partner, 0)
-
-    pl.semaphore_wait(barrier, total - 1)
-
-    for j in range(messages):
-        for k in range(1, nz + 1):
-            pa_move(j, k).start()
-    for k in near:
-        q_move(k).start()
-
-    for j in range(messages):
-
+        lax.fori_loop(1, nz + 1, for_partner, 0, unroll=1)
+
+    def sum_for_chips(batch):
         def for_chip(k, carry):
             owner = lax.rem(z_me + k, nz) * 2 + odd
-            sums = [partial_sum(first_pair(j, owner) + t) for t in range(held)]
-            pa_move(j, k).wait_recv()
-            block = part_in[j, k - 1]
-            for t, ((state, _), other) in enumerate(zip(sums, states_of(block))):
-                both[j, k - 1, t * size : (t + 1) * size, :] = (state + other).astype(jnp.bfloat16)
-            both[j, k - 1, base:, :] = split_mass([m + o for (_, m), o in zip(sums, masses_of(block))])
+            sums = {j: [partial_sum(first_pair(j, owner) + t) for t in range(held)] for j in batch}
+            for j in batch:
+                pa_move(j, k).wait_recv()
+            for j in batch:
+                block = part_in[j, k - 1]
+                for t, ((state, _), other) in enumerate(zip(sums[j], states_of(block))):
+                    both[j, k - 1, t * size : (t + 1) * size, :] = (state + other).astype(jnp.bfloat16)
+                both[j, k - 1, base:, :] = split_mass([m + o for (_, m), o in zip(sums[j], masses_of(block))])
 
             @pl.when(k < nz)
             def _():
-                rs_move(j, k).start()
+                rs_move(batch[0], k).start()
 
             return carry
 
-        lax.fori_loop(1, nz + 1, for_chip, 0)
+        lax.fori_loop(1, nz + 1, for_chip, 0, unroll=1)
+        for j in batch[1:]:
+            if j < messages - late:
+                for k in range(1, nz):
+                    rs_move(j, k).start()
+
+    def start_partner(batch):
+        for j in batch:
+            for k in range(1, nz + 1):
+                pa_move(j, k).start()
+
+    per = -(-nb // len(batches)) if spread else nb
+    for n, batch in enumerate(batches):
+        for i in range(n * per, min(n * per + per, nb)):
+            for copy in load(i):
+                copy.wait()
+        sum_for_partner(batch)
+        if n == 0:
+            pl.semaphore_wait(barrier, nb + nz - 1)
+        start_partner(batch)
+        if n == 0:
+            for k in near:
+                for m in range(PIECES):
+                    q_move(k, m).start()
+        sum_for_chips(batch)
 
     def features(k):
-        def featured(i, carry):
-            at = pl.multiple_of(i * LANES, LANES)
-            ft[k, i] = softplus(qx[k, pl.ds(at, LANES), :]).T
-            return carry
-
-        lax.fori_loop(0, ppg, featured, 0)
+        span = ppg // PIECES
+        for n in range(PIECES):
+            if k > 0:
+                q_move(back(k), n).wait_recv()
+
+            def featured(i, carry):
+                at = pl.multiple_of(i * LANES, LANES)
+                ft[k, i] = softplus(qx[k, pl.ds(at, LANES), :]).T
+                return carry
+
+            lax.fori_loop(n * span, (n + 1) * span, featured, 0, unroll=True)
 
     q_copy.wait()
     features(0)
@@ -206,11 +242,14 @@
         here, remote, local = ag_move(j, 0)
         pl.when(jnp.logical_not(here))(remote.start)
         pl.when(here)(local.start)
-        if j == 0:
+        if j == urgent - 1:
+            for i in range(messages - late, messages):
+                for k in range(1, nz):
+                    rs_move(i, k).start()
             for k in far:
-                q_move(k).start()
+                for n in range(EARLY, PIECES):
+                    q_move(k, n).start()
             for k in near:
-                q_move(back(k)).wait_recv()
                 features(k)
 
     def fw_move(k, u):
@@ -221,37 +260,44 @@
             device_id=(b, partner), device_id_type=MESH,
         )
 
-    def read(k, block):
-        at = ahead(k) * blocks + block
-        for t in range(held):
-            state = st[at, t * size : (t + 1) * size, :]
-            mass = st[at, base:, :].astype(jnp.float32)
-            mass = jnp.broadcast_to(mass[2 * t : 2 * t + 1], (size, LANES)).astype(jnp.bfloat16)
-            zero = jnp.zeros_like(state)
-            right = jnp.concatenate(
-                [jnp.where(lane, x, zero) if low else jnp.where(lane, zero, x)
-                 for x in (state, mass) for low in (True, False)], axis=0,
-            )
-            slot = block * held + t
-            y = lax.dot_general(
-                ft[k, slot], right, (((1,), (1,)), ((), ())), preferred_element_type=jnp.float32
-            )
+    def read(found):
+        products = []
+        for k, block in found:
+            at = ahead(k) * blocks + block
+            for t in range(held):
+                state = st[at, t * size : (t + 1) * size, :]
+                mass = st[at, base:, :].astype(jnp.float32)
+                mass = jnp.broadcast_to(mass[2 * t : 2 * t + 1], (size, LANES)).astype(jnp.bfloat16)
+                zero = jnp.zeros_like(state)
+                right = jnp.concatenate(
+                    [jnp.where(lane, x, zero) if low else jnp.where(lane, zero, x)
+                     for x in (state, mass) for low in (True, False)], axis=0,
+                )
+                slot = block * held + t
+                y = lax.dot_general(
+                    ft[k, slot], right, (((1,), (1,)), ((), ())), preferred_element_type=jnp.float32
+                )
+                products.append((k, slot, y))
+        for k, slot, y in products:
             y = y[:, :LANES] * (count**0.5 / (y[:, LANES:] + 0.001))
             column = pl.multiple_of(slot * LANES, LANES)
             mixed[k * tokens : (k + 1) * tokens, pl.ds(column, LANES)] = y.astype(jnp.bfloat16)
 
     def read_all(sequences):
-        for u in range(blocks // 2):
-            for k in sequences:
+        found = [(k, u) for u in range(blocks // 2) for k in sequences]
+        step = max(1, 4 // held)
+        for n in range(0, len(found), step):
+            for k, u in found[n : n + step]:
                 at = ahead(k) * blocks + 2 * u + odd
                 pltpu.make_async_copy(st.at[at], st.at[at], ag_recv.at[at]).wait()
                 fw_move(k, u).start()
-                read(k, 2 * u + odd)
-        for u in range(blocks // 2):
-            for k in sequences:
+            read([(k, 2 * u + odd) for k, u in found[n : n + step]])
+        step = max(1, 8 // held)
+        for n in range(0, len(found), step):
+            for k, u in found[n : n + step]:
                 at = ahead(k) * blocks + 2 * u + 1 - odd
                 pltpu.make_async_copy(st.at[at], st.at[at], fw_recv.at[at]).wait()
-                read(k, 2 * u + 1 - odd)
+            read([(k, 2 * u + 1 - odd) for k, u in found[n : n + step]])
 
     read_all(near)
 
@@ -312,7 +358,6 @@
 
     send_rows(lambda n2: [0])
     for k in far:
-        q_move(back(k)).wait_recv()
         features(k)
     read_all(far)
     send_rows(lambda n2: range(1, n2))
@@ -350,7 +395,8 @@
     lax.fori_loop(0, chunks, collect, 0)
 
     for k in range(1, nb):
-        q_move(k).wait_send()
+        for n in range(PIECES):
+            q_move(k, n).wait_send()
 
     for j in range(messages):
         for k in range(1, nz + 1):
@@ -403,6 +449,7 @@
         half_pairs, ppg = nc // 2, pairs // nb
         spread = nb % 2 == 0 and ppg % half_pairs == 0 and ppg >= half_pairs
         held = ppg // half_pairs if spread else 1
+        rounds = 1
         messages = pairs // nc // held
         high = held * size + EXTRA
         hops = pltpu.VMEM((messages, nc // 2, high, LANES), bf16)
@@ -423,8 +470,9 @@
             [stage((n1 - 1) * n2, (n1 - 1) * n2) for n1, n2 in sizes],
             [stage(n2 - 1, n2 - 1) for _, n2 in sizes],
             dma((4,)),
-            dma((nb,)),
-            dma((nb,)),
+            dma((2, nb)),
+            dma((nb, PIECES)),
+            dma((nb, PIECES)),
             dma((messages, nc // 2)),
             dma((messages, nc // 2)),
             dma((messages, nc // 2)),
@@ -439,7 +487,7 @@
         limit = used + 4 * tokens * columns + 3 * 2**20
 
         out = pl.pallas_call(
-            functools.partial(kernel, ny, nx, nc, size, (messages, held, spread)),
+            functools.partial(kernel, ny, nx, nc, size, (messages, held, rounds, spread)),
             out_shape=jax.ShapeDtypeStruct((tokens, columns), bf16),
             in_specs=[pl.BlockSpec(memory_space=pl.ANY)] * 4,
             out_specs=pl.BlockSpec(memory_space=pltpu.VMEM),

time: 61 us -> 59.5 us (0.975)
  Pallas kernels: 59.8 us -> 58.4 us
    pallas_call x1, Pallas kernels: 59.8 us -> 58.4 us  [shards(): pl.pallas_call(functools.partial(kernel, ny, nx, nc, size, (messages, hel...]
where the time goes in v3:
time: 59.5 us; the launch traced here: 59.4 us
  Pallas kernels  58.4 us (98%)
  local copies, waits for them, and re-layouts  0.97 us (2%)
    pallas_call x1, Pallas kernels, shards(): pl.pallas_call(functools.partial(kernel, ny, nx, nc, size, (messages, hel...  58.4 us

profile of v3, /device:TPU:0, one launch (start us, length us, event | category | flops | bytes accessed | tf_op | source)
XLA Modules:
  0.0 59.4 jit_solution(13495454564325070320)
XLA Ops:
  0.0 58.4 %shard_map.46 = bf16[128,4096]{1,0:T(8,128)(2,1)S(1)} custom-call(bf16[4096,128]{1,0:T(8,128)(2,1)} %bitcast.11, bf16[4096,128]{1,0:T(8,128)(2,1)} %bitcast.12, bf16[4096,128]{1,0:T(8,128)(2,1)} %bitcast.13, bf16[1024,4096]{1,0:T(8,128)(2,1)} %w_ref.1), custom_call_target="tpu_custom_call" | custom-call | tf_op jit(solution)/shard_map/pallas_call | solution.py:489
  58.4 1.0 %copy.6 = bf16[1,128,4096]{2,1,0:T(8,128)(2,1)} copy(bf16[1,128,4096]{2,1,0:T(8,128)(2,1)S(1)} %bitcast.10) | data formatting | bytes 2097152

commit v4 on v3

--- a/solution.py
+++ b/solution.py
@@ -11,9 +11,8 @@
 MESH = pl.DeviceIdType.MESH
 LANES = 128
 EXTRA = 8
-CHUNK = 512
+CHUNK = 1024
 PIECES = 4
-EARLY = 0
 
 
 def softplus(x):
@@ -25,7 +24,7 @@
     ny, nx, nc, size, grid, q_ref, k_ref, v_ref, w_ref, o_ref,
     kt, vt, wv, qx, ft, part, part_in, both, rs, own, st, mixed, mine, stage1, stage2,
     local_sem, load_sem, q_send, q_recv, pa_send, pa_recv, rs_send, rs_recv,
-    ag_send, ag_recv, fw_send, fw_recv,
+    ag_send, ag_recv, fw_send, fw_recv, relay_send,
 ):
     b, c = lax.axis_index("batch"), lax.axis_index("ctx")
     nb = ny * nx
@@ -78,7 +77,8 @@
     for k in range(1, nz):
         greet((b, lax.rem(c + 2 * k, nc)))
 
-    piece = share // PIECES
+    pieces = math.gcd(PIECES, ppg)
+    piece = share // pieces
 
     def q_move(k, n):
         to = ahead(k)
@@ -100,8 +100,15 @@
             return group * ppg + (owner // 2 * rounds + j % rounds) * held
         return j * nc + owner
 
-    urgent = min(rounds, messages) if spread else 1
-    late = 1 if messages > urgent and rounds > 1 else 0
+    urgent = rounds if spread and len(near) <= 2 * rounds else messages
+    late = order[2 * urgent :] if urgent < messages else []
+
+    def hop(i):
+        down, up = nz - 1 - i, i
+        down = jnp.where(down <= z_me, down - 1, down)
+        up = jnp.where(up >= z_me, up + 1, up)
+        k = lax.rem(jnp.where(2 * z_me < nz, down, up) - z_me + nz, nz)
+        return jnp.where(i == nz - 1, nz, k)
 
     def pa_move(j, k):
         return pltpu.make_async_remote_copy(
@@ -141,7 +148,8 @@
     batches = [range(j, min(j + rounds, messages)) for j in range(0, messages, rounds)]
 
     def sum_for_partner(batch):
-        def for_partner(k, carry):
+        def for_partner(i, carry):
+            k = hop(i)
             owner = lax.rem(z_me + k, nz) * 2 + 1 - odd
             for j in batch:
                 sums = [partial_sum(first_pair(j, owner) + t) for t in range(held)]
@@ -150,10 +158,11 @@
                 part[j, k - 1, base:, :] = split_mass([m for _, m in sums])
             return carry
 
-        lax.fori_loop(1, nz + 1, for_partner, 0, unroll=1)
+        lax.fori_loop(0, nz, for_partner, 0)
 
     def sum_for_chips(batch):
-        def for_chip(k, carry):
+        def for_chip(i, carry):
+            k = hop(i)
             owner = lax.rem(z_me + k, nz) * 2 + odd
             sums = {j: [partial_sum(first_pair(j, owner) + t) for t in range(held)] for j in batch}
             for j in batch:
@@ -164,22 +173,22 @@
                     both[j, k - 1, t * size : (t + 1) * size, :] = (state + other).astype(jnp.bfloat16)
                 both[j, k - 1, base:, :] = split_mass([m + o for (_, m), o in zip(sums[j], masses_of(block))])
 
-            @pl.when(k < nz)
+            @pl.when(i < nz - 1)
             def _():
                 rs_move(batch[0], k).start()
 
             return carry
 
-        lax.fori_loop(1, nz + 1, for_chip, 0, unroll=1)
+        lax.fori_loop(0, nz, for_chip, 0)
         for j in batch[1:]:
-            if j < messages - late:
+            if True:
                 for k in range(1, nz):
                     rs_move(j, k).start()
 
     def start_partner(batch):
         for j in batch:
-            for k in range(1, nz + 1):
-                pa_move(j, k).start()
+            for i in range(nz):
+                pa_move(j, hop(i)).start()
 
     per = -(-nb // len(batches)) if spread else nb
     for n, batch in enumerate(batches):
@@ -192,13 +201,13 @@
         start_partner(batch)
         if n == 0:
             for k in near:
-                for m in range(PIECES):
+                for m in range(pieces):
                     q_move(k, m).start()
         sum_for_chips(batch)
 
     def features(k):
-        span = ppg // PIECES
-        for n in range(PIECES):
+        span = ppg // pieces
+        for n in range(pieces):
             if k > 0:
                 q_move(back(k), n).wait_recv()
 
@@ -237,20 +246,34 @@
         for t, state in enumerate(states):
             own[j, t * size : (t + 1) * size, :] = state.astype(jnp.bfloat16)
         own[j, base:, :] = split_mass([jnp.broadcast_to(m, (EXTRA, LANES)) for m in masses])
-        for k in range(1, nz):
-            ag_move(j, k)[1].start()
+        for i in range(nz - 1 if j < urgent else 0):
+            ag_move(j, hop(i))[1].start()
         here, remote, local = ag_move(j, 0)
         pl.when(jnp.logical_not(here))(remote.start)
         pl.when(here)(local.start)
         if j == urgent - 1:
-            for i in range(messages - late, messages):
-                for k in range(1, nz):
-                    rs_move(i, k).start()
             for k in far:
-                for n in range(EARLY, PIECES):
+                for n in range(pieces):
                     q_move(k, n).start()
             for k in near:
                 features(k)
+
+    relays = lax.rem(z_me, 2) == odd
+
+    def relay_move(k, i):
+        landing = ahead(k) * blocks + z_me
+        return pltpu.make_async_remote_copy(
+            src_ref=st.at[landing], dst_ref=st.at[landing],
+            send_sem=relay_send.at[k, i], recv_sem=ag_recv.at[landing],
+            device_id=(b, lax.rem(z_me + hop(i), nz) * 2 + odd), device_id_type=MESH,
+        )
+
+    def relay_states():
+        for k in late:
+            at = ahead(k) * blocks + z_me
+            pltpu.make_async_copy(st.at[at], st.at[at], ag_recv.at[at]).wait()
+            for i in range(nz - 1):
+                relay_move(k, i).start()
 
     def fw_move(k, u):
         landing = ahead(k) * blocks + 2 * u + odd
@@ -289,7 +312,11 @@
         for n in range(0, len(found), step):
             for k, u in found[n : n + step]:
                 at = ahead(k) * blocks + 2 * u + odd
-                pltpu.make_async_copy(st.at[at], st.at[at], ag_recv.at[at]).wait()
+                arrival = pltpu.make_async_copy(st.at[at], st.at[at], ag_recv.at[at])
+                if k in late:
+                    pl.when(2 * u + odd != z_me)(arrival.wait)
+                else:
+                    arrival.wait()
                 fw_move(k, u).start()
             read([(k, 2 * u + odd) for k, u in found[n : n + step]])
         step = max(1, 8 // held)
@@ -357,6 +384,7 @@
         return carry
 
     send_rows(lambda n2: [0])
+    pl.when(relays)(relay_states)
     for k in far:
         features(k)
     read_all(far)
@@ -395,7 +423,7 @@
     lax.fori_loop(0, chunks, collect, 0)
 
     for k in range(1, nb):
-        for n in range(PIECES):
+        for n in range(pieces):
             q_move(k, n).wait_send()
 
     for j in range(messages):
@@ -403,12 +431,19 @@
             pa_move(j, k).wait_send()
         for k in range(1, nz):
             rs_move(j, k).wait_send()
-            ag_move(j, k)[1].wait_send()
+            if j < urgent:
+                ag_move(j, k)[1].wait_send()
         here, remote, _ = ag_move(j, 0)
         pl.when(jnp.logical_not(here))(remote.wait_send)
     for k in range(nb):
         for u in range(blocks // 2):
             fw_move(k, u).wait_send()
+
+    @pl.when(relays)
+    def _():
+        for k in late:
+            for i in range(nz - 1):
+                relay_move(k, i).wait_send()
 
     def pr_end(j, carry):
         for h, (n1, n2) in enumerate(sizes):
@@ -471,8 +506,8 @@
             [stage(n2 - 1, n2 - 1) for _, n2 in sizes],
             dma((4,)),
             dma((2, nb)),
-            dma((nb, PIECES)),
-            dma((nb, PIECES)),
+            dma((nb, math.gcd(PIECES, ppg))),
+            dma((nb, math.gcd(PIECES, ppg))),
             dma((messages, nc // 2)),
             dma((messages, nc // 2)),
             dma((messages, nc // 2)),
@@ -481,6 +516,7 @@
             dma((pairs // held,)),
             dma((pairs // held,)),
             dma((pairs // held,)),
+            dma((nb, nc // 2)),
         ]
         buffers = [x for x in jax.tree.leaves(scratch, is_leaf=lambda x: hasattr(x, "shape")) if x.dtype in (bf16, f32)]
         used = sum(math.prod(x.shape) * jnp.dtype(x.dtype).itemsize for x in buffers)

time: 59.5 us -> 58.7 us (0.987)
  Pallas kernels: 58.4 us -> 57.2 us
    pallas_call x1, Pallas kernels: 58.4 us -> 57.2 us  [shards(): pl.pallas_call(functools.partial(kernel, ny, nx, nc, size, (messages, hel...]
where the time goes in v4:
time: 58.7 us; the launch traced here: 58.2 us
  Pallas kernels  57.2 us (97%)
  local copies, waits for them, and re-layouts  0.97 us (2%)
    pallas_call x1, Pallas kernels, shards(): pl.pallas_call(functools.partial(kernel, ny, nx, nc, size, (messages, hel...  57.2 us

profile of v4, /device:TPU:0, one launch (start us, length us, event | category | flops | bytes accessed | tf_op | source)
XLA Modules:
  0.0 58.2 jit_solution(11775000749196155051)
XLA Ops:
  0.0 57.2 %shard_map.46 = bf16[128,4096]{1,0:T(8,128)(2,1)S(1)} custom-call(bf16[4096,128]{1,0:T(8,128)(2,1)} %bitcast.11, bf16[4096,128]{1,0:T(8,128)(2,1)} %bitcast.12, bf16[4096,128]{1,0:T(8,128)(2,1)} %bitcast.13, bf16[1024,4096]{1,0:T(8,128)(2,1)} %w_ref.1), custom_call_target="tpu_custom_call" | custom-call | tf_op jit(solution)/shard_map/pallas_call | solution.py:525
  57.2 1.0 %copy.6 = bf16[1,128,4096]{2,1,0:T(8,128)(2,1)} copy(bf16[1,128,4096]{2,1,0:T(8,128)(2,1)S(1)} %bitcast.10) | data formatting | bytes 2097152

commit v5 on v4

--- a/solution.py
+++ b/solution.py
@@ -12,7 +12,7 @@
 LANES = 128
 EXTRA = 8
 CHUNK = 1024
-PIECES = 4
+PIECES = 1
 
 
 def softplus(x):
@@ -60,11 +60,11 @@
 
     q_copy = pltpu.make_async_copy(q_ref.at[pl.ds(b * share, share)], qx.at[0], local_sem.at[2])
     w_copy = pltpu.make_async_copy(w_ref, wv, local_sem.at[3])
-    for i in range(nb):
+    batches = [range(j, min(j + rounds, messages)) for j in range(0, messages, rounds)]
+    per = -(-nb // len(batches)) if spread else nb
+    for i in range(per):
         for copy in load(i):
             copy.start()
-    q_copy.start()
-    w_copy.start()
 
     barrier = pltpu.get_barrier_semaphore()
 
@@ -145,7 +145,6 @@
         extra = block[base:].astype(jnp.float32)
         return [extra[2 * t : 2 * t + 1] + extra[2 * t + 1 : 2 * t + 2] for t in range(held)]
 
-    batches = [range(j, min(j + rounds, messages)) for j in range(0, messages, rounds)]
 
     def sum_for_partner(batch):
         def for_partner(i, carry):
@@ -190,11 +189,15 @@
             for i in range(nz):
                 pa_move(j, hop(i)).start()
 
-    per = -(-nb // len(batches)) if spread else nb
     for n, batch in enumerate(batches):
         for i in range(n * per, min(n * per + per, nb)):
             for copy in load(i):
                 copy.wait()
+        if n == 0:
+            for i in range(per, nb):
+                for copy in load(i):
+                    copy.start()
+            q_copy.start()
         sum_for_partner(batch)
         if n == 0:
             pl.semaphore_wait(barrier, nb + nz - 1)
@@ -204,6 +207,8 @@
                 for m in range(pieces):
                     q_move(k, m).start()
         sum_for_chips(batch)
+        if n == 0:
+            w_copy.start()
 
     def features(k):
         span = ppg // pieces
@@ -252,11 +257,11 @@
         pl.when(jnp.logical_not(here))(remote.start)
         pl.when(here)(local.start)
         if j == urgent - 1:
+            for k in near:
+                features(k)
             for k in far:
                 for n in range(pieces):
                     q_move(k, n).start()
-            for k in near:
-                features(k)
 
     relays = lax.rem(z_me, 2) == odd
 

time: 58.7 us -> 58.3 us (level)
  no operation moved by 1% of the time
where the time goes in v5:
time: 58.3 us; the launch traced here: 58.1 us
  Pallas kernels  57.2 us (98%)
  local copies, waits for them, and re-layouts  0.97 us (2%)
    pallas_call x1, Pallas kernels, shards(): pl.pallas_call(functools.partial(kernel, ny, nx, nc, size, (messages, hel...  57.2 us

profile of v5, /device:TPU:0, one launch (start us, length us, event | category | flops | bytes accessed | tf_op | source)
XLA Modules:
  0.0 58.1 jit_solution(1883308999534096521)
XLA Ops:
  0.0 57.2 %shard_map.46 = bf16[128,4096]{1,0:T(8,128)(2,1)S(1)} custom-call(bf16[4096,128]{1,0:T(8,128)(2,1)} %bitcast.11, bf16[4096,128]{1,0:T(8,128)(2,1)} %bitcast.12, bf16[4096,128]{1,0:T(8,128)(2,1)} %bitcast.13, bf16[1024,4096]{1,0:T(8,128)(2,1)} %w_ref.1), custom_call_target="tpu_custom_call" | custom-call | tf_op jit(solution)/shard_map/pallas_call | solution.py:530
  57.2 1.0 %copy.6 = bf16[1,128,4096]{2,1,0:T(8,128)(2,1)} copy(bf16[1,128,4096]{2,1,0:T(8,128)(2,1)S(1)} %bitcast.10) | data formatting | bytes 2097152

commit v6 on v5

--- a/solution.py
+++ b/solution.py
@@ -251,11 +251,11 @@
         for t, state in enumerate(states):
             own[j, t * size : (t + 1) * size, :] = state.astype(jnp.bfloat16)
         own[j, base:, :] = split_mass([jnp.broadcast_to(m, (EXTRA, LANES)) for m in masses])
-        for i in range(nz - 1 if j < urgent else 0):
-            ag_move(j, hop(i))[1].start()
         here, remote, local = ag_move(j, 0)
         pl.when(jnp.logical_not(here))(remote.start)
         pl.when(here)(local.start)
+        for i in range(nz - 1 if j < urgent else 0):
+            ag_move(j, hop(i))[1].start()
         if j == urgent - 1:
             for k in near:
                 features(k)

time: 58.3 us -> 58.3 us (level)
  no operation moved by 1% of the time
where the time goes in v6:
time: 58.3 us; the launch traced here: 58.1 us
  Pallas kernels  57.1 us (98%)
  local copies, waits for them, and re-layouts  0.97 us (2%)
    pallas_call x1, Pallas kernels, shards(): pl.pallas_call(functools.partial(kernel, ny, nx, nc, size, (messages, hel...  57.1 us

profile of v6, /device:TPU:0, one launch (start us, length us, event | category | flops | bytes accessed | tf_op | source)
XLA Modules:
  0.0 58.1 jit_solution(6738313961209118403)
XLA Ops:
  0.0 57.1 %shard_map.46 = bf16[128,4096]{1,0:T(8,128)(2,1)S(1)} custom-call(bf16[4096,128]{1,0:T(8,128)(2,1)} %bitcast.11, bf16[4096,128]{1,0:T(8,128)(2,1)} %bitcast.12, bf16[4096,128]{1,0:T(8,128)(2,1)} %bitcast.13, bf16[1024,4096]{1,0:T(8,128)(2,1)} %w_ref.1), custom_call_target="tpu_custom_call" | custom-call | tf_op jit(solution)/shard_map/pallas_call | solution.py:530
  57.2 1.0 %copy.6 = bf16[1,128,4096]{2,1,0:T(8,128)(2,1)} copy(bf16[1,128,4096]{2,1,0:T(8,128)(2,1)S(1)} %bitcast.10) | data formatting | bytes 2097152
